TPU v7x, 32 devices: a whole 2x2x4 slice. The times are simulated.
32 devices in a mesh: gx: 4 (over y, core), gy: 4 (over z), gz: 2 (over x).
Axes of the slice: x: 2, y: 2, z: 4, core: 2. Of those that a mesh axis runs over, the one named last changes fastest.
Arguments:
- moments: float32 [8, 16, 64, 1024], P(None, 'gx', 'gy', 'gz'), may hold values from 0.001 to 60, as said below
- velocity: float32 [3, 16, 64, 1024], P(None, 'gx', 'gy', 'gz'), may hold values from -4 to 4
- drift: float32 [3, 16, 64, 1024], P(None, 'gx', 'gy', 'gz'), may hold values from -8 to 8
Outputs:
- updated: float32 [8, 16, 64, 1024], P(None, 'gx', 'gy', 'gz')
- totals: float32 [8], replicated
Inputs may be any that keep to these rules, and one draw needn't show every extreme that they name: In every cell the 8 entries are the moments of order 0 to 7 of a log-normal distribution of particle size.
All inputs are finite; a program needn't handle non-finite values. Where the computation divides by a largest or mean magnitude, that divisor is 1e-20 or more.
Results may differ from a plain program's by a relative error of at most 0.0003.
Values sent between devices are 32-bit elements; how exact they have to be, the bound alone decides.
A program may use at most 64 MiB of HBM per device.

v0:
```python
import jax
import jax.numpy as jnp
from jax import lax
from jax.sharding import PartitionSpec as P

SWEEPS = 6


cfl_number = 0.4
speed_eps = 1e-06
pair_list = ((0, 1), (0, 2), (0, 3), (1, 2), (1, 3), (2, 3))


def padded(shard, sides, width, wrap):
    for axis, dim in sides:
        count, length = (lax.axis_size(axis), shard.shape[dim])
        up = [(i, (i + 1) % count) for i in range(count if wrap else count - 1)]
        down = [(j, i) for i, j in up]
        last = lax.slice_in_dim(shard, length - width, length, axis=dim)
        leading = lax.slice_in_dim(shard, 0, width, axis=dim)
        before = lax.ppermute(last, axis, up)
        after = lax.ppermute(leading, axis, down)
        shard = jnp.concatenate([before, shard, after], axis=dim)
    return shard


def entry_key(first_index, second_index):
    return (min(first_index, second_index), max(first_index, second_index))


def invert(moment):
    levels = [moment[order] for order in range(8)]
    zeros = jnp.zeros_like(levels[0])
    before = [zeros] * 8
    alphas = [levels[1] / levels[0]]
    betas = [levels[0]]
    for level in range(1, 4):
        fresh = [zeros] * 8
        for column in range(level, 8 - level):
            fresh[column] = (
                levels[column + 1]
                - alphas[level - 1] * levels[column]
                - betas[level - 1] * before[column]
            )
        alphas.append(fresh[level + 1] / fresh[level] - levels[level] / levels[level - 1])
        betas.append(fresh[level] / levels[level - 1])
        before, levels = (levels, fresh)
    table = {}
    for row_index in range(4):
        for col_index in range(row_index, 4):
            table[row_index, col_index] = zeros
    for row_index in range(4):
        table[row_index, row_index] = alphas[row_index]
    for row_index in range(3):
        table[row_index, row_index + 1] = jnp.sqrt(betas[row_index + 1])
    first = [jnp.ones_like(zeros), zeros, zeros, zeros]
    for _ in range(SWEEPS):
        for pivot, other in pair_list:
            coupling = table[pivot, other]
            head = table[pivot, pivot]
            tail = table[other, other]
            spread = tail - head
            orient = jnp.where(spread >= 0, 1.0, -1.0)
            tangent = (
                orient
                * 2.0
                * coupling
                / (jnp.abs(spread) + jnp.sqrt(spread * spread + 4.0 * coupling * coupling))
            )
            cosine = 1.0 / jnp.sqrt(1.0 + tangent * tangent)
            sine = tangent * cosine
            for rest in range(4):
                if rest != pivot and rest != other:
                    near = table[entry_key(rest, pivot)]
                    far = table[entry_key(rest, other)]
                    table[entry_key(rest, pivot)] = cosine * near - sine * far
                    table[entry_key(rest, other)] = sine * near + cosine * far
            table[pivot, pivot] = head - tangent * coupling
            table[other, other] = tail + tangent * coupling
            table[pivot, other] = jnp.zeros_like(coupling)
            first_p = first[pivot]
            first_q = first[other]
            first[pivot] = cosine * first_p - sine * first_q
            first[other] = sine * first_p + cosine * first_q
    weights = [moment[0] * first[node] * first[node] for node in range(4)]
    places = [table[node, node] for node in range(4)]
    return jnp.stack(weights + places)


def face_flux(extended, axis, count):

    def part(channel, start):
        return lax.slice_in_dim(extended[channel], start, start + count + 1, axis=axis - 1)

    mean_speed = 0.5 * (part(8, 0) + part(8, 1))
    mean_drift = 0.5 * (part(9, 0) + part(9, 1))
    zeros = jnp.zeros_like(mean_speed)
    accum = [zeros] * 8
    for node in range(4):
        for start, upwind in ((0, jnp.maximum), (1, jnp.minimum)):
            size = part(4 + node, start)
            carried = part(node, start) * upwind(mean_speed + mean_drift * size, 0.0)
            for order in range(8):
                accum[order] = accum[order] + carried
                carried = carried * size
    return jnp.stack(accum)


def shards(moments, velocity, drift):
    counts = moments.shape
    cells_total = (
        counts[1]
        * lax.axis_size("gx")
        * counts[2]
        * lax.axis_size("gy")
        * counts[3]
        * lax.axis_size("gz")
    )
    bottom = lax.axis_index("gz") == 0
    top = lax.axis_index("gz") == lax.axis_size("gz") - 1
    nodes = invert(moments)
    packs = [
        jnp.concatenate(
            [nodes, velocity[direction : direction + 1], drift[direction : direction + 1]], 0
        )
        for direction in range(3)
    ]
    extended_x = padded(packs[0], (("gx", 1),), 1, True)
    extended_y = padded(packs[1], (("gy", 2),), 1, True)
    extended_z = padded(packs[2], (("gz", 3),), 1, False)
    change = jnp.zeros_like(moments)
    for direction, extended in ((0, extended_x), (1, extended_y), (2, extended_z)):
        axis = direction + 1
        count = counts[axis]
        flux = face_flux(extended, axis, count)
        if direction == 2:
            face = lax.broadcasted_iota(jnp.int32, flux.shape, 3)
            wall = (face == 0) & bottom | (face == count) & top
            flux = jnp.where(wall, 0.0, flux)
        change = (
            change
            + lax.slice_in_dim(flux, 1, count + 1, axis=axis)
            - lax.slice_in_dim(flux, 0, count, axis=axis)
        )
    speed = jnp.zeros_like(moments[0])
    for direction in range(3):
        speed = speed + jnp.max(
            jnp.abs(velocity[direction][None] + drift[direction][None] * nodes[4:8]), axis=0
        )
    local_max = jnp.max(speed)
    global_max = lax.pmax(local_max, ("gx", "gy", "gz"))
    step_size = cfl_number / (global_max + speed_eps)
    updated = moments - step_size * change
    sums = lax.psum(jnp.sum(updated, axis=(1, 2, 3)), ("gx", "gy", "gz"))
    totals = sums / cells_total
    return (updated, totals)


def solution(mesh):
    in_specs = (P(None, "gx", "gy", "gz"), P(None, "gx", "gy", "gz"), P(None, "gx", "gy", "gz"))
    out_specs = (P(None, "gx", "gy", "gz"), P())
    return jax.shard_map(shards, mesh=mesh, in_specs=in_specs, out_specs=out_specs, check_vma=False)
```

profile of v0, /device:TPU:0, one launch (start us, length us, event | category | flops | bytes accessed | tf_op | source)
XLA Modules:
  0.0 132.4 jit_solution(10353812203924966196)
XLA Ops:
  0.6 1.1 subtract_subtract_fusion.4
  1.8 1.5 %divide_sqrt_fusion = (f32[1,4,16,512]{3,2,1,0:T(8,128)S(1)}, f32[1,4,16,512]{3,2,1,0:T(8,128)S(1)}, f32[1,4,16,512]{3,2,1,0:T(8,128)S(1)}, f32[1,4,16,512]{3,2,...) fusion(f32[8,4,16,512]{3,2,1,0:T(8,128)} %param.3, ...), kind=kLoop, calls=%fused_computation.610 | loop fusion | flops 1179648 | bytes 2228224 | tf_op jit(solution)/shard_map/sqrt | solution.py:55
  3.5 1.1 multiply_add_fusion.28
  5.5 0.9 multiply_add_fusion.23
  7.1 1.1 multiply_add_fusion.16
  8.2 0.8 multiply_subtract_fusion.105
  9.2 0.8 multiply_add_fusion.11
  10.3 0.8 multiply_add_fusion.44
  11.1 1.1 multiply_add_fusion.36
  12.8 0.6 multiply_multiply_fusion
  13.8 0.7 constant_dynamic-update-slice_fusion.18
  14.4 0.7 constant_dynamic-update-slice_fusion.17
  15.5 0.8 copy-done.4
  16.4 0.7 slice_bitcast_fusion.25
  17.4 0.8 slice_bitcast_fusion.24
  18.2 0.9 fusion.284
  19.6 1.9 %collective-permute-start.1 = (f32[10,1,16,512]{3,2,1,0:T(8,128)}, f32[10,1,16,512]{3,2,1,0:T(8,128)S(1)}, u32[]{:S(2)}, u32[]{:S(2)}) collective-permute-start(f32[10,1,16,512]{3,2,1,0:T(8,128)} %get-tuple-element.278), channel_id=1, source_target_pairs={{8,0},{16,8},{24,16},{0,24},{9,1},{17,9},{25,17},{1,25},{10,2},{18... | collective-permute-start | bytes 983048 | tf_op jit(solution)/shard_map/ppermute | solution.py:22
  21.6 0.8 fusion.285
  22.3 0.7 copy.31
  23.0 2.4 %collective-permute-start.2 = (f32[10,4,1,512]{3,0,2,1:T(8,128)}, f32[10,4,1,512]{3,0,2,1:T(8,128)}, u32[]{:S(2)}, u32[]{:S(2)}) collective-permute-start(f32[10,4,1,512]{3,0,2,1:T(8,128)} %copy.31), channel_id=1, source_target_pairs={{0,2},{2,4},{4,6},{6,0},{1,3},{3,5},{5,7},{7,1},{8,10},{10,12},{12... | collective-permute-start | bytes 245768 | tf_op jit(solution)/shard_map/ppermute | solution.py:21
  25.4 0.9 fusion.286
  26.3 4.1 %collective-permute-start.4 = (f32[10,4,16,1]{3,2,1,0:T(8,128)}, f32[10,4,16,1]{3,2,1,0:T(8,128)}, u32[]{:S(2)}, u32[]{:S(2)}) collective-permute-start(f32[10,4,16,1]{3,2,1,0:T(8,128)} %get-tuple-element.281), channel_id=1, source_target_pairs={{0,1},{2,3},{4,5},{6,7},{8,9},{10,11},{12,13},{14,15},{16,17},{18,... | collective-permute-start | bytes 7688 | tf_op jit(solution)/shard_map/ppermute | solution.py:21
  30.4 1.3 collective-permute-start.5
  31.7 1.4 %abs_reduce_fusion.1 = (f32[4,16,512]{2,1,0:T(8,128)S(1)}, f32[4,16,512]{2,1,0:T(8,128)S(1)}, f32[4,16,512]{2,1,0:T(8,128)S(1)}) fusion(f32[4,16,512]{2,1,0:T(8,128)} %get-tuple-element.293, f32[4,16,512]{2,1,0:T(8,128)} %get-tuple-element.287, f32[1,4,16,512]{3,2,1,0:T(8,128)S(1)} %get-tuple-element.61, f32[1,4,16,512]{3,2,1,0:T(8,128)} %get-tuple-element.63, ...), kind=kLoop, calls=%fused_computation.48 | loop fusion | flops 1867776 | bytes 1703936 | tf_op jit(solution)/shard_map/reduce_max | solution.py:147
  33.2 0.6 add_reduce_fusion
  33.8 42.5 %pmax.7 = f32[]{:T(128)} all-reduce(f32[]{:T(128)} %add_reduce_fusion), channel_id=1, replica_groups=mesh['gx'=4,'gy'=4,'gz'=2] {'gx','gy','gz'}, use_global_device_ids=true, to_apply=%region_4.5 | all-reduce | flops 1 | bytes 8 | tf_op jit(solution)/shard_map/pmax | solution.py:151
  76.3 0.9 copy.32
  77.9 2.3 %collective-permute-start.3 = (f32[10,4,1,512]{3,0,2,1:T(8,128)S(1)}, f32[10,4,1,512]{3,0,2,1:T(8,128)S(1)}, u32[]{:S(2)}, u32[]{:S(2)}) collective-permute-start(f32[10,4,1,512]{3,0,2,1:T(8,128)S(1)} %copy.32), channel_id=1, source_target_pairs={{2,0},{4,2},{6,4},{0,6},{3,1},{5,3},{7,5},{1,7},{10,8},{12,10},{14... | collective-permute-start | bytes 245768 | tf_op jit(solution)/shard_map/ppermute | solution.py:22
  80.2 2.0 %pad_maximum_fusion.1 = f32[10,4,16,514]{3,2,1,0:T(8,128)S(1)} fusion(f32[10,4,16,1]{3,2,1,0:T(8,128)} %collective-permute-done.5, f32[10,4,16,512]{3,2,1,0:T(8,128)} %copy-done.1, f32[10,4,16,1]{3,2,1,0:T(8,128)} %collective-permute-done.4), kind=kLoop, calls=%fused_computation.37 | loop fusion | flops 657920 | bytes 2631680 | tf_op jit(solution)/shard_map/concatenate | solution.py:23
  84.9 1.1 copy.33
  92.0 1.6 %fusion.223 = (f32[8]{0:T(128)S(1)}, f32[8,4,16,512]{3,2,1,0:T(8,128)}) fusion(f32[8,4,16,512]{3,2,1,0:T(8,128)S(1)} %copy-done, f32[8,4,16,513]{3,2,1,0:T(8,128)S(1)} %broadcast_select_fusion, f32[8,4,17,512]{3,2,1,0:T(8,128)S(1)} %bitcast_dynamic-update-slice_fusion, f32[8,5,16,512]{3,2,1,0:T(8,128)S(1)} %add_dynamic-update-slice_fusion, f32[]{:T(128)S(6)} %div.553), kind=kLoop, calls=%fused_computation.747 | loop fusion | flops 2097144 | bytes 8388644 | tf_op jit(solution)/shard_map/reduce_sum | solution.py:154
  93.6 38.3 %psum.7 = f32[8]{0:T(128)S(1)} all-reduce(f32[8]{0:T(128)S(1)} %get-tuple-element.5), channel_id=1, replica_groups=mesh['gx'=4,'gy'=4,'gz'=2] {'gx','gy','gz'}, use_global_device_ids=true, to_apply=%region_6.7 | all-reduce | flops 8 | bytes 64 | tf_op jit(solution)/shard_map/psum | solution.py:154
  (70 shorter events, 13.2 us)
Async XLA Ops:
  1.8 1.7 %copy-start = (f32[8,4,16,512]{3,2,1,0:T(8,128)S(1)}, f32[8,4,16,512]{3,2,1,0:T(8,128)}, u32[]{:S(2)}) copy-start(f32[8,4,16,512]{3,2,1,0:T(8,128)} %param.3) | copy-start | bytes 3145732
  15.4 1.0 copy-start.4
  16.4 1.0 copy-start.5
  18.2 7.2 %copy-start.1 = (f32[10,4,16,512]{3,2,1,0:T(8,128)}, f32[10,4,16,512]{3,2,1,0:T(8,128)S(1)}, u32[]{:S(2)}) copy-start(f32[10,4,16,512]{3,2,1,0:T(8,128)S(1)} %get-tuple-element.291) | copy-start | bytes 3932164
  18.2 8.2 %copy-start.2 = (f32[10,4,16,512]{3,2,1,0:T(8,128)}, f32[10,4,16,512]{3,2,1,0:T(8,128)S(1)}, u32[]{:S(2)}) copy-start(f32[10,4,16,512]{3,2,1,0:T(8,128)S(1)} %get-tuple-element.290) | copy-start | bytes 3932164
  19.1 70.2 %collective-permute-start = (f32[10,1,16,512]{3,2,1,0:T(8,128)}, f32[10,1,16,512]{3,2,1,0:T(8,128)S(1)}, u32[]{:S(2)}, u32[]{:S(2)}) collective-permute-start(f32[10,1,16,512]{3,2,1,0:T(8,128)} %get-tuple-element.277), channel_id=1, source_target_pairs={{0,8},{8,16},{16,24},{24,0},{1,9},{9,17},{17,25},{25,1},{2,10},{10... | collective-permute-start | bytes 983048 | tf_op jit(solution)/shard_map/ppermute | solution.py:21
  19.6 69.7 %collective-permute-start.1 = (f32[10,1,16,512]{3,2,1,0:T(8,128)}, f32[10,1,16,512]{3,2,1,0:T(8,128)S(1)}, u32[]{:S(2)}, u32[]{:S(2)}) collective-permute-start(f32[10,1,16,512]{3,2,1,0:T(8,128)} %get-tuple-element.278), channel_id=1, source_target_pairs={{8,0},{16,8},{24,16},{0,24},{9,1},{17,9},{25,17},{1,25},{10,2},{18... | collective-permute-start | bytes 983048 | tf_op jit(solution)/shard_map/ppermute | solution.py:22
  23.0 61.8 %collective-permute-start.2 = (f32[10,4,1,512]{3,0,2,1:T(8,128)}, f32[10,4,1,512]{3,0,2,1:T(8,128)}, u32[]{:S(2)}, u32[]{:S(2)}) collective-permute-start(f32[10,4,1,512]{3,0,2,1:T(8,128)} %copy.31), channel_id=1, source_target_pairs={{0,2},{2,4},{4,6},{6,0},{1,3},{3,5},{5,7},{7,1},{8,10},{10,12},{12... | collective-permute-start | bytes 245768 | tf_op jit(solution)/shard_map/ppermute | solution.py:21
  26.3 51.6 %collective-permute-start.4 = (f32[10,4,16,1]{3,2,1,0:T(8,128)}, f32[10,4,16,1]{3,2,1,0:T(8,128)}, u32[]{:S(2)}, u32[]{:S(2)}) collective-permute-start(f32[10,4,16,1]{3,2,1,0:T(8,128)} %get-tuple-element.281), channel_id=1, source_target_pairs={{0,1},{2,3},{4,5},{6,7},{8,9},{10,11},{12,13},{14,15},{16,17},{18,... | collective-permute-start | bytes 7688 | tf_op jit(solution)/shard_map/ppermute | solution.py:21
  30.4 49.8 %collective-permute-start.5 = (f32[10,4,16,1]{3,2,1,0:T(8,128)}, f32[10,4,16,1]{3,2,1,0:T(8,128)}, u32[]{:S(2)}, u32[]{:S(2)}) collective-permute-start(f32[10,4,16,1]{3,2,1,0:T(8,128)} %get-tuple-element.282), channel_id=1, source_target_pairs={{1,0},{3,2},{5,4},{7,6},{9,8},{11,10},{13,12},{15,14},{17,16},{19,... | collective-permute-start | bytes 7688 | tf_op jit(solution)/shard_map/ppermute | solution.py:22
  77.9 8.1 %collective-permute-start.3 = (f32[10,4,1,512]{3,0,2,1:T(8,128)S(1)}, f32[10,4,1,512]{3,0,2,1:T(8,128)S(1)}, u32[]{:S(2)}, u32[]{:S(2)}) collective-permute-start(f32[10,4,1,512]{3,0,2,1:T(8,128)S(1)} %copy.32), channel_id=1, source_target_pairs={{2,0},{4,2},{6,4},{0,6},{3,1},{5,3},{7,5},{1,7},{10,8},{12,10},{14... | collective-permute-start | bytes 245768 | tf_op jit(solution)/shard_map/ppermute | solution.py:22
  84.7 1.4 %copy-start.3 = (f32[10,4,16,512]{3,2,1,0:T(8,128)S(1)}, f32[10,4,16,512]{3,2,1,0:T(8,128)}, u32[]{:S(2)}) copy-start(f32[10,4,16,512]{3,2,1,0:T(8,128)} %copy-done.2) | copy-start | bytes 3932164
where the time goes:
time: 133 us; the launch traced here: 132 us
  blocking collectives  80.8 us (61%)
  other arithmetic  28.5 us (21%)
  starting transfers between devices  12.5 us (9%)
  local copies, waits for them, and re-layouts  8.81 us (7%)
  between operations  1.79 us (1%)
    pmax x1, blocking collectives, shards(): global_max = lax.pmax(local_max, ('gx', 'gy', 'gz'))  42.5 us
    psum x1, blocking collectives, shards(): sums = lax.psum(jnp.sum(updated, axis=(1, 2, 3)), ('gx', 'gy', 'gz'))  38.3 us
    unnamed x25, other arithmetic  7.93 us
    ppermute x3, starting transfers between devices, padded(): before = lax.ppermute(last, axis, up)  6.95 us
    ppermute x3, starting transfers between devices, padded(): after = lax.ppermute(leading, axis, down)  5.55 us
    add x5, other arithmetic, invert(): first[other] = sine * first_p + cosine * first_q  4.27 us
    slice x4, local copies, waits for them, and re-layouts, padded(): last = lax.slice_in_dim(shard, length - width, length, axis=dim)  3.34 us
    add x5, other arithmetic, invert(): table[entry_key(rest, other)] = sine * near + cosine * far  2.86 us
  transfers between devices with their start and end apart: 6, of which 0 were waited for; matrix products, arithmetic and copies ran while one was open for 11% of the time, Pallas kernels for 0%

commit v1 on v0

v1 whole, which is shorter than its diff:
```python
import functools

import jax
import jax.numpy as jnp
from jax import lax
from jax.experimental import pallas as pl
from jax.experimental.pallas import tpu as pltpu
from jax.sharding import PartitionSpec as P

SWEEPS = 6
AXES = ("gx", "gy", "gz")
JACOBI_LANES = 256
LANES = 128

cfl_number = 0.4
speed_eps = 1e-06
pair_list = ((0, 1), (0, 2), (0, 3), (1, 2), (1, 3), (2, 3))


def entry_key(i, j):
    return (min(i, j), max(i, j))


def rotated(cosine, sine, near, far):
    if near is None and far is None:
        return None, None
    if near is None:
        return -(sine * far), cosine * far
    if far is None:
        return cosine * near, sine * near
    return cosine * near - sine * far, sine * near + cosine * far


def invert(moment):
    levels = list(moment)
    before = None
    inverse = 1.0 / levels[0]
    ratios = [levels[1] * inverse]
    alphas = [ratios[0]]
    betas = [levels[0]]
    for level in range(1, 4):
        fresh = [None] * 8
        for column in range(level, 8 - level):
            value = levels[column + 1] - alphas[level - 1] * levels[column]
            if level > 1:
                value = value - betas[level - 1] * before[column]
            fresh[column] = value
        betas.append(fresh[level] * inverse)
        inverse = 1.0 / fresh[level]
        ratios.append(fresh[level + 1] * inverse)
        alphas.append(ratios[level] - ratios[level - 1])
        before, levels = levels, fresh
    table = {(i, j): None for i in range(4) for j in range(i, 4)}
    for i in range(4):
        table[i, i] = alphas[i]
    for i in range(3):
        table[i, i + 1] = jnp.sqrt(betas[i + 1])
    first = [1.0, None, None, None]
    for _ in range(SWEEPS):
        for p, q in pair_list:
            coupling = table[p, q]
            if coupling is None:
                continue
            spread = table[q, q] - table[p, p]
            double = coupling + coupling
            r = lax.rsqrt(spread * spread + double * double)
            c2 = 0.5 + 0.5 * (jnp.abs(spread) * r)
            rc = lax.rsqrt(c2)
            cosine = c2 * rc
            signed = jnp.where(spread >= 0, coupling, -coupling)
            sine = signed * (r * rc)
            shift = sine * rc * coupling
            for rest in range(4):
                if rest not in (p, q):
                    a, b = entry_key(rest, p), entry_key(rest, q)
                    table[a], table[b] = rotated(cosine, sine, table[a], table[b])
            table[p, p] = table[p, p] - shift
            table[q, q] = table[q, q] + shift
            table[p, q] = None
            first[p], first[q] = rotated(cosine, sine, first[p], first[q])
    weights = [moment[0] * first[i] * first[i] for i in range(4)]
    return weights, [table[i, i] for i in range(4)]


def outflow(weights, sizes, mean_speed, mean_drift, upwind):
    sums = None
    for w, s in zip(weights, sizes):
        term = w * upwind(mean_speed + mean_drift * s, 0.0)
        terms = [term]
        for _ in range(7):
            term = term * s
            terms.append(term)
        sums = terms if sums is None else [a + b for a, b in zip(sums, terms)]
    return sums


def kernel(
    sizes, m_hbm, v_hbm, g_hbm, out_hbm, tot_ref,
    m, v, g, nodes, acc, out, xp, xm, zp, zm,
    hvx, vy_s, vy_r, vz_s, vz_r, y_s, y_r, z_s, z_r, peak, total,
    in_sem, out_sem, nb_send, nb_recv, all_send, all_recv,
):
    X, Y, Z = m.shape[1:]
    count = sizes[0] * sizes[1] * sizes[2]
    at = [lax.axis_index(a) for a in AXES]
    me = (at[0] * sizes[1] + at[1]) * sizes[2] + at[2]
    row = lax.broadcasted_iota(jnp.int32, (Y, LANES), 0)
    lane = lax.broadcasted_iota(jnp.int32, (Y, LANES), 1)
    bottom = at[2] == 0
    top = at[2] == sizes[2] - 1

    def peer(offset):
        where = lax.rem(me + offset, count)
        return (
            where // (sizes[1] * sizes[2]),
            lax.rem(where // sizes[2], sizes[1]),
            lax.rem(where, sizes[2]),
        )

    def beside(axis, step):
        place = list(at)
        place[axis] = lax.rem(at[axis] + step + sizes[axis], sizes[axis])
        return tuple(place)

    loads = [pltpu.make_async_copy(m_hbm.at[:, x], m.at[:, x], in_sem.at[x]) for x in range(X)]
    loads_v = pltpu.make_async_copy(v_hbm, v, in_sem.at[X])
    loads_g = pltpu.make_async_copy(g_hbm, g, in_sem.at[X + 1])
    loads_v.start()
    loads_g.start()
    edge = [0] if X == 1 else [0, X - 1]
    inner = list(range(1, X - 1))
    for x in edge + inner:
        loads[x].start()

    barrier = pltpu.get_barrier_semaphore()

    def greet(offset, carry):
        pl.semaphore_signal(
            barrier, inc=1, device_id=peer(offset), device_id_type=pl.DeviceIdType.MESH
        )
        return carry

    lax.fori_loop(1, count, greet, 0)

    sent = []

    def send(src, dst, axis, step):
        index = len(sent)
        copy = pltpu.make_async_remote_copy(
            src_ref=src, dst_ref=dst, send_sem=nb_send.at[index], recv_sem=nb_recv.at[index],
            device_id=beside(axis, step), device_id_type=pl.DeviceIdType.MESH,
        )
        copy.start()
        sent.append(copy)
        return copy

    loads_v.wait()
    loads_g.wait()
    for x in range(X):
        for part, ref in ((0, v), (1, g)):
            vy_s[0, x, part : part + 1, :] = ref[1, x, Y - 1 : Y, :]
            vy_s[1, x, part : part + 1, :] = ref[1, x, 0:1, :]
        high = [ref[2, x, :, Z - LANES : Z] for ref in (v, g)]
        low = [ref[2, x, :, 0:LANES] for ref in (v, g)]
        vz_s[0, x] = jnp.where(lane == 0, pltpu.roll(high[0], 1, 1), pltpu.roll(high[1], 2, 1))
        vz_s[1, x] = jnp.where(lane == 0, low[0], pltpu.roll(low[1], 1, 1))

    pl.semaphore_wait(barrier, count - 1)
    velocity_copies = [
        send(v.at[0, X - 1], hvx.at[0, 0], 0, 1),
        send(g.at[0, X - 1], hvx.at[0, 1], 0, 1),
        send(v.at[0, 0], hvx.at[1, 0], 0, -1),
        send(g.at[0, 0], hvx.at[1, 1], 0, -1),
        send(vy_s.at[0], vy_r.at[0], 1, 1),
        send(vy_s.at[1], vy_r.at[1], 1, -1),
        send(vz_s.at[0], vz_r.at[0], 2, 1),
        send(vz_s.at[1], vz_r.at[1], 2, -1),
    ]

    chunks = Z // JACOBI_LANES

    def solve(x, chunk, best):
        zs = pl.ds(pl.multiple_of(chunk * JACOBI_LANES, JACOBI_LANES), JACOBI_LANES)
        weights, places = invert([m[k, x, :, zs] for k in range(8)])
        for i in range(4):
            nodes[i, x, :, zs] = weights[i]
            nodes[4 + i, x, :, zs] = places[i]
        speed = None
        for d in range(3):
            vd, gd = v[d, x, :, zs], g[d, x, :, zs]
            parts = [jnp.abs(vd + gd * s) for s in places]
            largest = jnp.maximum(
                jnp.maximum(parts[0], parts[1]), jnp.maximum(parts[2], parts[3])
            )
            speed = largest if speed is None else speed + largest
        return jnp.maximum(best, speed)

    best = jnp.zeros((Y, JACOBI_LANES), jnp.float32)
    for x in edge:
        loads[x].wait()
    best = lax.fori_loop(
        0, len(edge) * chunks,
        lambda i, b: solve(lax.div(i, chunks) * (X - 1), lax.rem(i, chunks), b), best,
    )

    for copy in velocity_copies[:4]:
        copy.wait_recv()

    def lanes_of(chunk):
        return pl.ds(pl.multiple_of(chunk * LANES, LANES), LANES)

    def nodes_of(x, zs):
        return (
            [nodes[i, x, :, zs] for i in range(4)], [nodes[4 + i, x, :, zs] for i in range(4)]
        )

    def edge_x(chunk, carry):
        zs = lanes_of(chunk)
        w, s = nodes_of(X - 1, zs)
        speed = 0.5 * (v[0, X - 1, :, zs] + hvx[1, 0, :, zs])
        slope = 0.5 * (g[0, X - 1, :, zs] + hvx[1, 1, :, zs])
        for k, value in enumerate(outflow(w, s, speed, slope, jnp.maximum)):
            xp[X, k, :, zs] = value
        w, s = nodes_of(0, zs)
        speed = 0.5 * (v[0, 0, :, zs] + hvx[0, 0, :, zs])
        slope = 0.5 * (g[0, 0, :, zs] + hvx[0, 1, :, zs])
        for k, value in enumerate(outflow(w, s, speed, slope, jnp.minimum)):
            xm[0, k, :, zs] = value
        return carry

    lax.fori_loop(0, Z // LANES, edge_x, 0)
    x_copies = [
        send(xp.at[X], xp.at[0], 0, 1),
        send(xm.at[0], xm.at[X], 0, -1),
    ]

    for x in inner:
        loads[x].wait()
    if inner:
        best = lax.fori_loop(
            0, len(inner) * chunks,
            lambda i, b: solve(lax.div(i, chunks) + 1, lax.rem(i, chunks), b), best,
        )

    best = jnp.max(best, axis=0, keepdims=True)
    best = functools.reduce(
        jnp.maximum, [best[:, i : i + LANES] for i in range(0, JACOBI_LANES, LANES)]
    )
    peak[0] = best

    def spread_copy(buffer, which, offset):
        return pltpu.make_async_remote_copy(
            src_ref=buffer.at[0], dst_ref=buffer.at[offset],
            send_sem=all_send.at[which, offset], recv_sem=all_recv.at[which, offset],
            device_id=peer(offset), device_id_type=pl.DeviceIdType.MESH,
        )

    def spread(buffer, which):
        def one(offset, carry):
            spread_copy(buffer, which, offset).start()
            return carry

        lax.fori_loop(1, count, one, 0)

    def gathered(buffer, which):
        def one(offset, carry):
            spread_copy(buffer, which, offset).wait_recv()
            return carry

        lax.fori_loop(1, count, one, 0)

    for copy in velocity_copies[4:]:
        copy.wait_recv()

    zc = Z // LANES

    def side_faces(i, carry):
        x, chunk = lax.div(i, zc), lax.rem(i, zc)
        zs = lanes_of(chunk)
        w, s = nodes_of(x, zs)
        vy, gy = v[1, x, :, zs], g[1, x, :, zs]
        up = [
            jnp.where(row == Y - 1, vy_r[1, x, part : part + 1, zs], pltpu.roll(a, Y - 1, 0))
            for part, a in ((0, vy), (1, gy))
        ]
        down = [
            jnp.where(row == 0, vy_r[0, x, part : part + 1, zs], pltpu.roll(a, 1, 0))
            for part, a in ((0, vy), (1, gy))
        ]
        high = outflow(w, s, 0.5 * (vy + up[0]), 0.5 * (gy + up[1]), jnp.maximum)
        for k in range(8):
            y_s[0, x, k : k + 1, zs] = high[k][Y - 1 : Y, :]
            acc[x, k, :, zs] = high[k] - jnp.where(row == 0, 0.0, pltpu.roll(high[k], 1, 0))
        low = outflow(w, s, 0.5 * (vy + down[0]), 0.5 * (gy + down[1]), jnp.minimum)
        for k in range(8):
            y_s[1, x, k : k + 1, zs] = low[k][0:1, :]
            acc[x, k, :, zs] += (
                jnp.where(row == Y - 1, 0.0, pltpu.roll(low[k], Y - 1, 0)) - low[k]
            )
        return carry

    lax.fori_loop(0, X * zc, side_faces, 0)
    spread(peak, 0)
    y_copies = [send(y_s.at[0], y_r.at[0], 1, 1), send(y_s.at[1], y_r.at[1], 1, -1)]

    def wall_faces(i, carry):
        x, chunk = lax.div(i, zc), lax.rem(i, zc)
        zs = lanes_of(chunk)
        nxt = lanes_of(lax.rem(chunk + 1, zc))
        prv = lanes_of(lax.rem(chunk + zc - 1, zc))
        w, s = nodes_of(x, zs)
        final = chunk == zc - 1
        start = chunk == 0

        def means(ref, part):
            here = ref[2, x, :, zs]
            after = jnp.where(final, pltpu.roll(vz_r[1, x], LANES - part, 1), ref[2, x, :, nxt])
            ahead = jnp.where(
                start, pltpu.roll(vz_r[0, x], LANES - 1 - part, 1), ref[2, x, :, prv]
            )
            up = jnp.where(
                lane == LANES - 1, pltpu.roll(after, LANES - 1, 1), pltpu.roll(here, LANES - 1, 1)
            )
            down = jnp.where(lane == 0, pltpu.roll(ahead, 1, 1), pltpu.roll(here, 1, 1))
            return 0.5 * (here + up), 0.5 * (here + down)

        speeds, slopes = means(v, 0), means(g, 1)
        shut_high = (lane == LANES - 1) & (final & top)
        shut_low = (lane == 0) & (start & bottom)
        high = outflow(w, s, speeds[0], slopes[0], jnp.maximum)
        for k in range(8):
            zp[x, k, :, zs] = jnp.where(shut_high, 0.0, high[k])
        low = outflow(w, s, speeds[1], slopes[1], jnp.minimum)
        for k in range(8):
            zm[x, k, :, zs] = jnp.where(shut_low, 0.0, low[k])
        return carry

    lax.fori_loop(0, X * zc, wall_faces, 0)

    def pack_z(x, carry):
        high = jnp.zeros((Y, LANES), jnp.float32)
        low = jnp.zeros((Y, LANES), jnp.float32)
        for k in range(8):
            high = jnp.where(
                lane == k, pltpu.roll(zp[x, k, :, Z - LANES : Z], k + 1, 1), high
            )
            column = zm[x, k, :, 0:LANES]
            low = jnp.where(lane == k, pltpu.roll(column, k, 1) if k else column, low)
        z_s[0, x] = high
        z_s[1, x] = low
        return carry

    lax.fori_loop(0, X, pack_z, 0)

    def inner_x(i, carry):
        x, chunk = lax.div(i, zc), lax.rem(i, zc)
        zs = lanes_of(chunk)
        speed = 0.5 * (v[0, x, :, zs] + v[0, x + 1, :, zs])
        slope = 0.5 * (g[0, x, :, zs] + g[0, x + 1, :, zs])
        w, s = nodes_of(x, zs)
        left = outflow(w, s, speed, slope, jnp.maximum)
        for k in range(8):
            xp[x + 1, k, :, zs] = left[k]
        w, s = nodes_of(x + 1, zs)
        right = outflow(w, s, speed, slope, jnp.minimum)
        for k in range(8):
            xm[x + 1, k, :, zs] = right[k]
        return carry

    z_copies = [send(z_s.at[0], z_r.at[0], 2, 1), send(z_s.at[1], z_r.at[1], 2, -1)]
    if X > 1:
        lax.fori_loop(0, (X - 1) * zc, inner_x, 0)

    gathered(peak, 0)
    largest = jnp.max(jnp.max(peak[...], axis=0), axis=1, keepdims=True)
    step = cfl_number / (largest + speed_eps)

    for copy in x_copies + y_copies + z_copies:
        copy.wait_recv()

    wide_row = lax.broadcasted_iota(jnp.int32, (Y, Z), 0)
    wide_lane = lax.broadcasted_iota(jnp.int32, (Y, Z), 1)

    def combine(x, sums):
        fresh = []
        low_all, high_all = z_r[0, x], z_r[1, x]
        for k in range(8):
            fp, fm = zp[x, k], zm[x, k]
            before = jnp.where(wide_lane == 0, 0.0, pltpu.roll(fp, 1, 1))
            after = jnp.where(wide_lane == Z - 1, 0.0, pltpu.roll(fm, Z - 1, 1))
            change = acc[x, k] + ((fp + after) - (fm + before))
            change = change + ((xp[x + 1, k] + xm[x + 1, k]) - (xp[x, k] + xm[x, k]))
            change = change + jnp.where(
                wide_row == Y - 1, y_r[1, x, k : k + 1, :],
                jnp.where(wide_row == 0, -y_r[0, x, k : k + 1, :], 0.0),
            )
            out[k, x] = m[k, x] - step * change
            first = jnp.where(lane == 0, pltpu.roll(low_all, LANES - k, 1) if k else low_all, 0.0)
            last = jnp.where(lane == LANES - 1, pltpu.roll(high_all, LANES - 1 - k, 1), 0.0)
            out[k, x, :, 0:LANES] += step * first
            out[k, x, :, Z - LANES : Z] -= step * last
            value = out[k, x]
            fold = functools.reduce(
                jnp.add, [value[i : i + 8, :] for i in range(0, Y, 8)]
            )
            fold = functools.reduce(
                jnp.add, [fold[:, i : i + LANES] for i in range(0, Z, LANES)]
            )
            fresh.append(sums[k] + fold)
        pltpu.make_async_copy(out.at[:, x], out_hbm.at[:, x], out_sem.at[x]).start()
        return tuple(fresh)

    zero = jnp.zeros((8, LANES), jnp.float32)
    sums = lax.fori_loop(0, X, combine, (zero,) * 8)

    one_lane = lax.broadcasted_iota(jnp.int32, (1, LANES), 1)
    packed = jnp.zeros((1, LANES), jnp.float32)
    for k in range(8):
        value = jnp.sum(jnp.sum(sums[k], axis=0, keepdims=True), axis=1, keepdims=True)
        packed = jnp.where(one_lane == k, value, packed)
    total[0] = packed
    spread(total, 1)
    gathered(total, 1)
    tot_ref[...] = jnp.sum(total[...], axis=0) / float(count * X * Y * Z)

    for x in range(X):
        pltpu.make_async_copy(out.at[:, x], out_hbm.at[:, x], out_sem.at[x]).wait()
    for copy in sent:
        copy.wait_send()

    def drain(offset, carry):
        for which, buffer in ((0, peak), (1, total)):
            spread_copy(buffer, which, offset).wait_send()
        return carry

    lax.fori_loop(1, count, drain, 0)


def shards(sizes, moments, velocity, drift):
    _, X, Y, Z = moments.shape
    count = sizes[0] * sizes[1] * sizes[2]
    f32 = jnp.float32
    vm = lambda *shape: pltpu.VMEM(shape, f32)
    updated, totals = pl.pallas_call(
        functools.partial(kernel, sizes),
        name="transport",
        out_shape=(
            jax.ShapeDtypeStruct(moments.shape, f32), jax.ShapeDtypeStruct((1, LANES), f32)
        ),
        in_specs=[pl.BlockSpec(memory_space=pl.ANY)] * 3,
        out_specs=(
            pl.BlockSpec(memory_space=pl.ANY), pl.BlockSpec(memory_space=pltpu.VMEM)
        ),
        scratch_shapes=[
            vm(8, X, Y, Z), vm(3, X, Y, Z), vm(3, X, Y, Z), vm(8, X, Y, Z), vm(X, 8, Y, Z),
            vm(8, X, Y, Z), vm(X + 1, 8, Y, Z), vm(X + 1, 8, Y, Z), vm(X, 8, Y, Z),
            vm(X, 8, Y, Z),
            vm(2, 2, Y, Z), vm(2, X, 2, Z), vm(2, X, 2, Z), vm(2, X, Y, LANES),
            vm(2, X, Y, LANES), vm(2, X, 8, Z), vm(2, X, 8, Z), vm(2, X, Y, LANES),
            vm(2, X, Y, LANES), vm(count, 1, LANES), vm(count, 1, LANES),
            pltpu.SemaphoreType.DMA((X + 2,)), pltpu.SemaphoreType.DMA((X,)),
            pltpu.SemaphoreType.DMA((14,)), pltpu.SemaphoreType.DMA((14,)),
            pltpu.SemaphoreType.DMA((2, count)), pltpu.SemaphoreType.DMA((2, count)),
        ],
        compiler_params=pltpu.CompilerParams(collective_id=0, has_side_effects=True),
    )(moments, velocity, drift)
    return updated, totals[0, :8]


def solution(mesh):
    spec = P(None, "gx", "gy", "gz")
    sizes = tuple(mesh.shape[a] for a in AXES)
    return jax.shard_map(
        functools.partial(shards, sizes), mesh=mesh, in_specs=(spec,) * 3,
        out_specs=(spec, P()), check_vma=False,
    )
```

time: 133 us -> 34.6 us (0.26)
  blocking collectives: 80.8 us -> 0 us
  Pallas kernels: 0 us -> 30.3 us
  other arithmetic: 28.5 us -> 0 us
  starting transfers between devices: 12.5 us -> 0 us
  local copies, waits for them, and re-layouts: 8.81 us -> 3.43 us
    pmax x1 -> x0, blocking collectives: 42.5 us -> none  [shards(): global_max = lax.pmax(local_max, ('gx', 'gy', 'gz'))]
    psum x1 -> x0, blocking collectives: 38.3 us -> none  [shards(): sums = lax.psum(jnp.sum(updated, axis=(1, 2, 3)), ('gx', 'gy', 'gz'))]
    pallas_call x0 -> x1, Pallas kernels: none -> 30.3 us  [shards(): pl.pallas_call(functools.partial(kernel, sizes), name='transport', out_sh...]
    ppermute x6 -> x0, starting transfers between devices: 12.5 us -> none  [the longest x3 6.95 us: padded(): before = lax.ppermute(last, axis, up)]
    unnamed x25 -> x0, other arithmetic: 7.93 us -> none
    add x10 -> x0, other arithmetic: 7.13 us -> none  [the longest x5 4.27 us: invert(): first[other] = sine * first_p + cosine * first_q]
    slice x5 -> x0, local copies, waits for them, and re-layouts: 4.26 us -> none  [the longest x4 3.34 us: padded(): last = lax.slice_in_dim(shard, length - width, length, axis=dim)]
    sub x4 -> x0, other arithmetic: 2.56 us -> none  [the longest x1 1.14 us: invert(): levels[column + 1] - alphas[level - 1] * levels[column]]
  transfers between devices with their start and end apart: 6 -> 0, of which waited for: 0 -> 0; matrix products, arithmetic and copies ran while one was open for 11% -> 0% of each run, Pallas kernels for 0% -> 0%
where the time goes in v1:
time: 34.6 us; the launch traced here: 34.4 us
  Pallas kernels  30.3 us (88%)
  local copies, waits for them, and re-layouts  3.43 us (10%)
  between operations  0.65 us (2%)
    pallas_call x1, Pallas kernels, shards(): pl.pallas_call(functools.partial(kernel, sizes), name='transport', out_sh...  30.3 us
    unnamed x3, local copies, waits for them, and re-layouts  2.92 us

profile of v1, /device:TPU:0, one launch (start us, length us, event | category | flops | bytes accessed | tf_op | source)
XLA Modules:
  0.0 34.4 jit_solution(6243792505615686082)
XLA Ops:
  0.6 30.3 %transport.1 = (f32[8,4,16,512]{3,2,1,0:T(8,128)}, f32[1,128]{1,0:T(1,128)}) custom-call(f32[8,4,16,512]{3,2,1,0:T(8,128)} %m_hbm.1, f32[3,4,16,512]{3,2,1,0:T(8,128)} %v_hbm.1, f32[3,4,16,512]{3,2,1,0:T(8,128)} %g_hbm.1), custom_call_target="tpu_custom_call" | custom-call | tf_op jit(solution)/shard_map/transport/pallas_call | solution.py:444
  31.0 0.0 copy-start
  31.0 0.6 %copy-done = f32[1,128]{1,0:T(1,128)S(1)} copy-done((f32[1,128]{1,0:T(1,128)S(1)}, f32[1,128]{1,0:T(1,128)}, u32[]{:S(2)}) %copy-start) | copy-done | bytes 536
  31.6 0.5 %slice_bitcast_fusion = f32[8]{0:T(128)} fusion(f32[1,128]{1,0:T(1,128)S(1)} %copy-done), kind=kLoop, calls=%fused_computation | loop fusion | bytes 64 | tf_op jit(solution)/shard_map/squeeze | solution.py:467
  32.1 2.3 %copy.6 = f32[8,4,16,512]{3,2,1,0:T(8,128)} copy(f32[8,4,16,512]{3,2,1,0:T(8,128)} %get-tuple-element.8) | data formatting | bytes 2097152
Async XLA Ops:
  31.0 0.6 %copy-start = (f32[1,128]{1,0:T(1,128)S(1)}, f32[1,128]{1,0:T(1,128)}, u32[]{:S(2)}) copy-start(f32[1,128]{1,0:T(1,128)} %get-tuple-element.5) | copy-start | bytes 1540

commit v2 on v1

--- a/solution.py
+++ b/solution.py
@@ -95,10 +95,10 @@
 
 
 def kernel(
-    sizes, m_hbm, v_hbm, g_hbm, out_hbm, tot_ref,
-    m, v, g, nodes, acc, out, xp, xm, zp, zm,
+    sizes, m_hbm, v_hbm, g_hbm, out, tot_ref,
+    m, v, g, nodes, acc, fx, zp, zm,
     hvx, vy_s, vy_r, vz_s, vz_r, y_s, y_r, z_s, z_r, peak, total,
-    in_sem, out_sem, nb_send, nb_recv, all_send, all_recv,
+    in_sem, nb_send, nb_recv, all_send, all_recv,
 ):
     X, Y, Z = m.shape[1:]
     count = sizes[0] * sizes[1] * sizes[2]
@@ -125,11 +125,12 @@
     loads = [pltpu.make_async_copy(m_hbm.at[:, x], m.at[:, x], in_sem.at[x]) for x in range(X)]
     loads_v = pltpu.make_async_copy(v_hbm, v, in_sem.at[X])
     loads_g = pltpu.make_async_copy(g_hbm, g, in_sem.at[X + 1])
+    edge = [0] if X == 1 else [0, X - 1]
+    inner = list(range(1, X - 1))
+    loads[0].start()
     loads_v.start()
     loads_g.start()
-    edge = [0] if X == 1 else [0, X - 1]
-    inner = list(range(1, X - 1))
-    for x in edge + inner:
+    for x in edge[1:] + inner:
         loads[x].start()
 
     barrier = pltpu.get_barrier_semaphore()
@@ -165,6 +166,30 @@
         vz_s[0, x] = jnp.where(lane == 0, pltpu.roll(high[0], 1, 1), pltpu.roll(high[1], 2, 1))
         vz_s[1, x] = jnp.where(lane == 0, low[0], pltpu.roll(low[1], 1, 1))
 
+    chunks = Z // JACOBI_LANES
+
+    def solve(x, chunk, best):
+        zs = pl.ds(pl.multiple_of(chunk * JACOBI_LANES, JACOBI_LANES), JACOBI_LANES)
+        weights, places = invert([m[k, x, :, zs] for k in range(8)])
+        for i in range(4):
+            nodes[x + 1, i, :, zs] = weights[i]
+            nodes[x + 1, 4 + i, :, zs] = places[i]
+        speed = None
+        for d in range(3):
+            vd, gd = v[d, x, :, zs], g[d, x, :, zs]
+            parts = [jnp.abs(vd + gd * s) for s in places]
+            largest = jnp.maximum(
+                jnp.maximum(parts[0], parts[1]), jnp.maximum(parts[2], parts[3])
+            )
+            speed = largest if speed is None else speed + largest
+        return jnp.maximum(best, speed)
+
+    best = jnp.zeros((Y, JACOBI_LANES), jnp.float32)
+    def solve_layer(x, best):
+        return lax.fori_loop(0, chunks, lambda i, b: solve(x, i, b), best)
+
+    loads[0].wait()
+    best = solve_layer(0, best)
     pl.semaphore_wait(barrier, count - 1)
     velocity_copies = [
         send(v.at[0, X - 1], hvx.at[0, 0], 0, 1),
@@ -176,63 +201,22 @@
         send(vz_s.at[0], vz_r.at[0], 2, 1),
         send(vz_s.at[1], vz_r.at[1], 2, -1),
     ]
-
-    chunks = Z // JACOBI_LANES
-
-    def solve(x, chunk, best):
-        zs = pl.ds(pl.multiple_of(chunk * JACOBI_LANES, JACOBI_LANES), JACOBI_LANES)
-        weights, places = invert([m[k, x, :, zs] for k in range(8)])
-        for i in range(4):
-            nodes[i, x, :, zs] = weights[i]
-            nodes[4 + i, x, :, zs] = places[i]
-        speed = None
-        for d in range(3):
-            vd, gd = v[d, x, :, zs], g[d, x, :, zs]
-            parts = [jnp.abs(vd + gd * s) for s in places]
-            largest = jnp.maximum(
-                jnp.maximum(parts[0], parts[1]), jnp.maximum(parts[2], parts[3])
-            )
-            speed = largest if speed is None else speed + largest
-        return jnp.maximum(best, speed)
-
-    best = jnp.zeros((Y, JACOBI_LANES), jnp.float32)
-    for x in edge:
-        loads[x].wait()
-    best = lax.fori_loop(
-        0, len(edge) * chunks,
-        lambda i, b: solve(lax.div(i, chunks) * (X - 1), lax.rem(i, chunks), b), best,
-    )
-
-    for copy in velocity_copies[:4]:
-        copy.wait_recv()
+    if X > 1:
+        loads[X - 1].wait()
+        best = solve_layer(X - 1, best)
+    x_copies = [
+        send(nodes.at[1], nodes.at[X + 1], 0, -1),
+        send(nodes.at[X], nodes.at[0], 0, 1),
+    ]
 
     def lanes_of(chunk):
         return pl.ds(pl.multiple_of(chunk * LANES, LANES), LANES)
 
-    def nodes_of(x, zs):
+    def nodes_of(layer, zs):
         return (
-            [nodes[i, x, :, zs] for i in range(4)], [nodes[4 + i, x, :, zs] for i in range(4)]
-        )
-
-    def edge_x(chunk, carry):
-        zs = lanes_of(chunk)
-        w, s = nodes_of(X - 1, zs)
-        speed = 0.5 * (v[0, X - 1, :, zs] + hvx[1, 0, :, zs])
-        slope = 0.5 * (g[0, X - 1, :, zs] + hvx[1, 1, :, zs])
-        for k, value in enumerate(outflow(w, s, speed, slope, jnp.maximum)):
-            xp[X, k, :, zs] = value
-        w, s = nodes_of(0, zs)
-        speed = 0.5 * (v[0, 0, :, zs] + hvx[0, 0, :, zs])
-        slope = 0.5 * (g[0, 0, :, zs] + hvx[0, 1, :, zs])
-        for k, value in enumerate(outflow(w, s, speed, slope, jnp.minimum)):
-            xm[0, k, :, zs] = value
-        return carry
-
-    lax.fori_loop(0, Z // LANES, edge_x, 0)
-    x_copies = [
-        send(xp.at[X], xp.at[0], 0, 1),
-        send(xm.at[0], xm.at[X], 0, -1),
-    ]
+            [nodes[layer, i, :, zs] for i in range(4)],
+            [nodes[layer, 4 + i, :, zs] for i in range(4)],
+        )
 
     for x in inner:
         loads[x].wait()
@@ -277,7 +261,7 @@
     def side_faces(i, carry):
         x, chunk = lax.div(i, zc), lax.rem(i, zc)
         zs = lanes_of(chunk)
-        w, s = nodes_of(x, zs)
+        w, s = nodes_of(x + 1, zs)
         vy, gy = v[1, x, :, zs], g[1, x, :, zs]
         up = [
             jnp.where(row == Y - 1, vy_r[1, x, part : part + 1, zs], pltpu.roll(a, Y - 1, 0))
@@ -308,7 +292,7 @@
         zs = lanes_of(chunk)
         nxt = lanes_of(lax.rem(chunk + 1, zc))
         prv = lanes_of(lax.rem(chunk + zc - 1, zc))
-        w, s = nodes_of(x, zs)
+        w, s = nodes_of(x + 1, zs)
         final = chunk == zc - 1
         start = chunk == 0
 
@@ -352,79 +336,95 @@
 
     lax.fori_loop(0, X, pack_z, 0)
 
+    def face_x(face, zs, left, right):
+        speed, slope = 0.5 * (left[0] + right[0]), 0.5 * (left[1] + right[1])
+        upper = outflow(*nodes_of(face, zs), speed, slope, jnp.maximum)
+        lower = outflow(*nodes_of(face + 1, zs), speed, slope, jnp.minimum)
+        for k in range(8):
+            fx[face, k, :, zs] = upper[k] + lower[k]
+
+    def drift_of(x, zs):
+        return v[0, x, :, zs], g[0, x, :, zs]
+
     def inner_x(i, carry):
-        x, chunk = lax.div(i, zc), lax.rem(i, zc)
-        zs = lanes_of(chunk)
-        speed = 0.5 * (v[0, x, :, zs] + v[0, x + 1, :, zs])
-        slope = 0.5 * (g[0, x, :, zs] + g[0, x + 1, :, zs])
-        w, s = nodes_of(x, zs)
-        left = outflow(w, s, speed, slope, jnp.maximum)
-        for k in range(8):
-            xp[x + 1, k, :, zs] = left[k]
-        w, s = nodes_of(x + 1, zs)
-        right = outflow(w, s, speed, slope, jnp.minimum)
-        for k in range(8):
-            xm[x + 1, k, :, zs] = right[k]
+        face, zs = lax.div(i, zc) + 1, lanes_of(lax.rem(i, zc))
+        face_x(face, zs, drift_of(face - 1, zs), drift_of(face, zs))
+        return carry
+
+    def outer_x(i, carry):
+        zs = lanes_of(i)
+        face_x(0, zs, (hvx[0, 0, :, zs], hvx[0, 1, :, zs]), drift_of(0, zs))
+        face_x(X, zs, drift_of(X - 1, zs), (hvx[1, 0, :, zs], hvx[1, 1, :, zs]))
         return carry
 
     z_copies = [send(z_s.at[0], z_r.at[0], 2, 1), send(z_s.at[1], z_r.at[1], 2, -1)]
     if X > 1:
         lax.fori_loop(0, (X - 1) * zc, inner_x, 0)
 
+    for copy in velocity_copies[:4] + x_copies:
+        copy.wait_recv()
+    lax.fori_loop(0, zc, outer_x, 0)
+    for copy in y_copies + z_copies:
+        copy.wait_recv()
+
+    wide_row = lax.broadcasted_iota(jnp.int32, (Y, Z), 0)
+    wide_lane = lax.broadcasted_iota(jnp.int32, (Y, Z), 1)
+
+    def fold(value):
+        value = functools.reduce(jnp.add, [value[i : i + 8, :] for i in range(0, Y, 8)])
+        return functools.reduce(jnp.add, [value[:, i : i + LANES] for i in range(0, Z, LANES)])
+
+    def combine(x, sums):
+        fresh = []
+        low_all, high_all = z_r[0, x], z_r[1, x]
+        for k in range(8):
+            fp, fm = zp[x, k], zm[x, k]
+            first = pltpu.roll(low_all, LANES - k, 1) if k else low_all
+            last = pltpu.roll(high_all, LANES - 1 - k, 1)
+            spare = [first] * (Z // LANES - 1)
+            before = jnp.where(
+                wide_lane == 0, jnp.concatenate([first] + spare, 1), pltpu.roll(fp, 1, 1)
+            )
+            spare = [last] * (Z // LANES - 1)
+            after = jnp.where(
+                wide_lane == Z - 1, jnp.concatenate(spare + [last], 1), pltpu.roll(fm, Z - 1, 1)
+            )
+            change = acc[x, k] + ((fp + after) - (fm + before))
+            change = change + (fx[x + 1, k] - fx[x, k])
+            change = change + jnp.where(
+                wide_row == Y - 1, y_r[1, x, k : k + 1, :],
+                jnp.where(wide_row == 0, -y_r[0, x, k : k + 1, :], 0.0),
+            )
+            acc[x, k] = change
+            fresh.append(sums[k] + fold(m[k, x]))
+            fresh.append(sums[8 + k] + fold(change))
+        return tuple(fresh[0::2] + fresh[1::2])
+
+    zero = jnp.zeros((8, LANES), jnp.float32)
+    sums = lax.fori_loop(0, X, combine, (zero,) * 16)
+
+    one_lane = lax.broadcasted_iota(jnp.int32, (1, LANES), 1)
+    packed = jnp.zeros((1, LANES), jnp.float32)
+    for k in range(16):
+        value = jnp.sum(jnp.sum(sums[k], axis=0, keepdims=True), axis=1, keepdims=True)
+        packed = jnp.where(one_lane == k, value, packed)
+    total[0] = packed
     gathered(peak, 0)
     largest = jnp.max(jnp.max(peak[...], axis=0), axis=1, keepdims=True)
     step = cfl_number / (largest + speed_eps)
-
-    for copy in x_copies + y_copies + z_copies:
-        copy.wait_recv()
-
-    wide_row = lax.broadcasted_iota(jnp.int32, (Y, Z), 0)
-    wide_lane = lax.broadcasted_iota(jnp.int32, (Y, Z), 1)
-
-    def combine(x, sums):
-        fresh = []
-        low_all, high_all = z_r[0, x], z_r[1, x]
-        for k in range(8):
-            fp, fm = zp[x, k], zm[x, k]
-            before = jnp.where(wide_lane == 0, 0.0, pltpu.roll(fp, 1, 1))
-            after = jnp.where(wide_lane == Z - 1, 0.0, pltpu.roll(fm, Z - 1, 1))
-            change = acc[x, k] + ((fp + after) - (fm + before))
-            change = change + ((xp[x + 1, k] + xm[x + 1, k]) - (xp[x, k] + xm[x, k]))
-            change = change + jnp.where(
-                wide_row == Y - 1, y_r[1, x, k : k + 1, :],
-                jnp.where(wide_row == 0, -y_r[0, x, k : k + 1, :], 0.0),
-            )
-            out[k, x] = m[k, x] - step * change
-            first = jnp.where(lane == 0, pltpu.roll(low_all, LANES - k, 1) if k else low_all, 0.0)
-            last = jnp.where(lane == LANES - 1, pltpu.roll(high_all, LANES - 1 - k, 1), 0.0)
-            out[k, x, :, 0:LANES] += step * first
-            out[k, x, :, Z - LANES : Z] -= step * last
-            value = out[k, x]
-            fold = functools.reduce(
-                jnp.add, [value[i : i + 8, :] for i in range(0, Y, 8)]
-            )
-            fold = functools.reduce(
-                jnp.add, [fold[:, i : i + LANES] for i in range(0, Z, LANES)]
-            )
-            fresh.append(sums[k] + fold)
-        pltpu.make_async_copy(out.at[:, x], out_hbm.at[:, x], out_sem.at[x]).start()
-        return tuple(fresh)
-
-    zero = jnp.zeros((8, LANES), jnp.float32)
-    sums = lax.fori_loop(0, X, combine, (zero,) * 8)
-
-    one_lane = lax.broadcasted_iota(jnp.int32, (1, LANES), 1)
-    packed = jnp.zeros((1, LANES), jnp.float32)
-    for k in range(8):
-        value = jnp.sum(jnp.sum(sums[k], axis=0, keepdims=True), axis=1, keepdims=True)
-        packed = jnp.where(one_lane == k, value, packed)
-    total[0] = packed
     spread(total, 1)
+
+    def update(x, carry):
+        for k in range(8):
+            out[k, x] = m[k, x] - step * acc[x, k]
+        return carry
+
+    lax.fori_loop(0, X, update, 0)
     gathered(total, 1)
-    tot_ref[...] = jnp.sum(total[...], axis=0) / float(count * X * Y * Z)
-
-    for x in range(X):
-        pltpu.make_async_copy(out.at[:, x], out_hbm.at[:, x], out_sem.at[x]).wait()
+    both = jnp.sum(total[...], axis=0)
+    both = both - step * pltpu.roll(jnp.broadcast_to(both, (8, LANES)), LANES - 8, 1)[0:1]
+    tot_ref[...] = both / float(count * X * Y * Z)
+
     for copy in sent:
         copy.wait_send()
 
@@ -445,20 +445,19 @@
         functools.partial(kernel, sizes),
         name="transport",
         out_shape=(
-            jax.ShapeDtypeStruct(moments.shape, f32), jax.ShapeDtypeStruct((1, LANES), f32)
+            pltpu.VMEM(moments.shape, f32), pltpu.VMEM((1, LANES), f32)
         ),
         in_specs=[pl.BlockSpec(memory_space=pl.ANY)] * 3,
         out_specs=(
-            pl.BlockSpec(memory_space=pl.ANY), pl.BlockSpec(memory_space=pltpu.VMEM)
+            pl.BlockSpec(memory_space=pltpu.VMEM), pl.BlockSpec(memory_space=pltpu.VMEM)
         ),
         scratch_shapes=[
-            vm(8, X, Y, Z), vm(3, X, Y, Z), vm(3, X, Y, Z), vm(8, X, Y, Z), vm(X, 8, Y, Z),
-            vm(8, X, Y, Z), vm(X + 1, 8, Y, Z), vm(X + 1, 8, Y, Z), vm(X, 8, Y, Z),
-            vm(X, 8, Y, Z),
+            vm(8, X, Y, Z), vm(3, X, Y, Z), vm(3, X, Y, Z), vm(X + 2, 8, Y, Z), vm(X, 8, Y, Z),
+            vm(X + 1, 8, Y, Z), vm(X, 8, Y, Z), vm(X, 8, Y, Z),
             vm(2, 2, Y, Z), vm(2, X, 2, Z), vm(2, X, 2, Z), vm(2, X, Y, LANES),
             vm(2, X, Y, LANES), vm(2, X, 8, Z), vm(2, X, 8, Z), vm(2, X, Y, LANES),
             vm(2, X, Y, LANES), vm(count, 1, LANES), vm(count, 1, LANES),
-            pltpu.SemaphoreType.DMA((X + 2,)), pltpu.SemaphoreType.DMA((X,)),
+            pltpu.SemaphoreType.DMA((X + 2,)),
             pltpu.SemaphoreType.DMA((14,)), pltpu.SemaphoreType.DMA((14,)),
             pltpu.SemaphoreType.DMA((2, count)), pltpu.SemaphoreType.DMA((2, count)),
         ],

time: 34.6 us -> 31 us (0.90)
  local copies, waits for them, and re-layouts: 3.43 us -> 1.48 us
  Pallas kernels: 30.3 us -> 28.7 us
    unnamed x3 -> x1, local copies, waits for them, and re-layouts: 2.92 us -> 0.97 us
    pallas_call x1, Pallas kernels: 30.3 us -> 28.7 us  [shards(): pl.pallas_call(functools.partial(kernel, sizes), name='transport', out_sh...]
where the time goes in v2:
time: 31 us; the launch traced here: 30.8 us
  Pallas kernels  28.7 us (93%)
  local copies, waits for them, and re-layouts  1.48 us (5%)
  between operations  0.64 us (2%)
    pallas_call x1, Pallas kernels, shards(): pl.pallas_call(functools.partial(kernel, sizes), name='transport', out_sh...  28.7 us
    unnamed x1, local copies, waits for them, and re-layouts  0.97 us

profile of v2, /device:TPU:0, one launch (start us, length us, event | category | flops | bytes accessed | tf_op | source)
XLA Modules:
  0.0 30.8 jit_solution(1305804629622271898)
XLA Ops:
  0.6 28.7 %transport.1 = (f32[8,4,16,512]{3,2,1,0:T(8,128)S(1)}, f32[1,128]{1,0:T(1,128)S(1)}) custom-call(f32[8,4,16,512]{3,2,1,0:T(8,128)} %m_hbm.1, f32[3,4,16,512]{3,2,1,0:T(8,128)} %v_hbm.1, f32[3,4,16,512]{3,2,1,0:T(8,128)} %g_hbm.1), custom_call_target="tpu_custom_call" | custom-call | tf_op jit(solution)/shard_map/transport/pallas_call | solution.py:444
  29.4 1.0 %copy.6 = f32[8,4,16,512]{3,2,1,0:T(8,128)} copy(f32[8,4,16,512]{3,2,1,0:T(8,128)S(1)} %get-tuple-element.6) | data formatting | bytes 2097152
  30.3 0.5 %slice_bitcast_fusion = f32[8]{0:T(128)} fusion(f32[1,128]{1,0:T(1,128)S(1)} %get-tuple-element.5), kind=kLoop, calls=%fused_computation | loop fusion | bytes 64 | tf_op jit(solution)/shard_map/squeeze | solution.py:466

commit v3 on v2

--- a/solution.py
+++ b/solution.py
@@ -9,7 +9,7 @@
 
 SWEEPS = 6
 AXES = ("gx", "gy", "gz")
-JACOBI_LANES = 256
+JACOBI_LANES = 512
 LANES = 128
 
 cfl_number = 0.4
@@ -409,10 +409,10 @@
         value = jnp.sum(jnp.sum(sums[k], axis=0, keepdims=True), axis=1, keepdims=True)
         packed = jnp.where(one_lane == k, value, packed)
     total[0] = packed
+    spread(total, 1)
     gathered(peak, 0)
     largest = jnp.max(jnp.max(peak[...], axis=0), axis=1, keepdims=True)
     step = cfl_number / (largest + speed_eps)
-    spread(total, 1)
 
     def update(x, carry):
         for k in range(8):

time: 31 us -> 30.1 us (0.971)
  Pallas kernels: 28.7 us -> 27.9 us
    pallas_call x1, Pallas kernels: 28.7 us -> 27.9 us  [shards(): pl.pallas_call(functools.partial(kernel, sizes), name='transport', out_sh...]
where the time goes in v3:
time: 30.1 us; the launch traced here: 30 us
  Pallas kernels  27.9 us (93%)
  local copies, waits for them, and re-layouts  1.48 us (5%)
  between operations  0.64 us (2%)
    pallas_call x1, Pallas kernels, shards(): pl.pallas_call(functools.partial(kernel, sizes), name='transport', out_sh...  27.9 us
    unnamed x1, local copies, waits for them, and re-layouts  0.97 us

profile of v3, /device:TPU:0, one launch (start us, length us, event | category | flops | bytes accessed | tf_op | source)
XLA Modules:
  0.0 30.0 jit_solution(6262719103450104338)
XLA Ops:
  0.6 27.9 %transport.1 = (f32[8,4,16,512]{3,2,1,0:T(8,128)S(1)}, f32[1,128]{1,0:T(1,128)S(1)}) custom-call(f32[8,4,16,512]{3,2,1,0:T(8,128)} %m_hbm.1, f32[3,4,16,512]{3,2,1,0:T(8,128)} %v_hbm.1, f32[3,4,16,512]{3,2,1,0:T(8,128)} %g_hbm.1), custom_call_target="tpu_custom_call" | custom-call | tf_op jit(solution)/shard_map/transport/pallas_call | solution.py:444
  28.5 1.0 %copy.6 = f32[8,4,16,512]{3,2,1,0:T(8,128)} copy(f32[8,4,16,512]{3,2,1,0:T(8,128)S(1)} %get-tuple-element.6) | data formatting | bytes 2097152
  29.5 0.5 %slice_bitcast_fusion = f32[8]{0:T(128)} fusion(f32[1,128]{1,0:T(1,128)S(1)} %get-tuple-element.5), kind=kLoop, calls=%fused_computation | loop fusion | bytes 64 | tf_op jit(solution)/shard_map/squeeze | solution.py:466
